TPU v7x, 32 devices: a whole 2x2x4 slice. The times are simulated.
32 devices in a mesh: vert: 4 (over y, x), feat: 8 (over z, core).
Axes of the slice: x: 2, y: 2, z: 4, core: 2. Of those that a mesh axis runs over, the one named last changes fastest.
Arguments:
- features: bfloat16 [32768, 256], P('vert', 'feat'), may hold values from -6 to 6
- tiles: bfloat16 [256, 16, 128, 128], P('vert'), may hold values from -0.1875 to 0.1875
- tile_cols: int32 [256, 16], P('vert'), may hold values from 0 to 79
- tile_count: int32 [256], P('vert'), may hold values from 1 to 16, as said below
- send_list: int32 [4, 4, 4], P('vert'), may hold values from 0 to 63
- weight: bfloat16 [256, 256], replicated, may hold values from -0.375 to 0.375
- bias: float32 [256], replicated, may hold values from -3 to 3
Outputs:
- node_out: bfloat16 [32768, 256], P(('vert', 'feat'))
Inputs may be any that keep to these rules, and one draw needn't show every extreme that they name: Row block r uses tile places 0 to tile_count[r] - 1; in every draw some row block uses all 16.
All inputs are finite; a program needn't handle non-finite values.
Results may differ from a plain program's by a relative error of at most 0.0044.
Values may be sent and summed in bfloat16 or wider, within the bound.
A program may use at most 128 MiB of HBM per device.

v0:
```python
import jax
import jax.numpy as jnp
from jax import lax
from jax.sharding import PartitionSpec as P


def add_tile(total, extended, tiles, tile_cols, tile_count, tile_slot):
    wanted = lax.dynamic_index_in_dim(tile_cols, tile_slot, 1, keepdims=False)
    picked = jnp.take(extended, wanted, axis=0)
    tile_page = lax.dynamic_index_in_dim(tiles, tile_slot, 1, keepdims=False)
    product = jnp.einsum("rcj,rij->cri", picked, tile_page, preferred_element_type=jnp.float32)
    is_live = tile_slot < tile_count
    return total + jnp.where(is_live[None, :, None], product, jnp.float32(0.0))


def per_device(features, tiles, tile_cols, tile_count, send_list, weight, bias):
    block_count = tiles.shape[0]
    tile_depth = tiles.shape[1]
    edge = tiles.shape[2]
    width = features.shape[1]
    vert_count = lax.axis_size("vert")
    slot_count = send_list.shape[2]
    blocks = jnp.transpose(features.reshape(block_count, edge, width), (0, 2, 1))
    chosen = jnp.take(blocks, send_list[0], axis=0)
    arrived = lax.all_to_all(chosen, "vert", split_axis=0, concat_axis=0, tiled=True)
    extended = jnp.concatenate(
        [blocks, arrived.reshape(vert_count * slot_count, width, edge)], axis=0
    )
    total = jnp.zeros((width, block_count, edge), jnp.float32)
    for tile_slot in range(tile_depth):
        total = add_tile(total, extended, tiles, tile_cols, tile_count, tile_slot)
    hidden = total.astype(jnp.bfloat16).reshape(width, block_count * edge)
    full_rows = lax.all_to_all(hidden, "feat", split_axis=1, concat_axis=0, tiled=True)
    mixed_rows = lax.dot_general(
        full_rows, weight, (((0,), (0,)), ((), ())), preferred_element_type=jnp.float32
    )
    return jnp.maximum(mixed_rows + bias, jnp.float32(0.0)).astype(jnp.bfloat16)


def solution(mesh):
    return jax.shard_map(
        per_device,
        mesh=mesh,
        in_specs=(
            P("vert", "feat"),
            P("vert", None, None, None),
            P("vert", None),
            P("vert"),
            P("vert", None, None),
            P(),
            P(),
        ),
        out_specs=P(("vert", "feat"), None),
        check_vma=False,
    )
```

profile of v0, /device:TPU:0, one launch (start us, length us, event | category | flops | bytes accessed | tf_op | source)
XLA Modules:
  0.0 102.8 jit_solution(10233807345983602473)
XLA Ops:
  0.0 0.0 copy-start
  0.0 0.7 compare_select_fusion
  0.7 0.7 compare_and_fusion.16
  1.4 0.0 copy-done
  1.4 0.1 bitcast_bitcast_fusion
  1.5 0.1 reshape.199
  1.6 0.6 gather_fusion
  2.2 0.7 broadcast_select_fusion
  2.9 5.2 %all-to-all-start = ((bf16[4,4,32,128]{3,2,1,0:T(8,128)(2,1)}), bf16[4,4,32,128]{3,2,1,0:T(8,128)(2,1)S(1)}, u32[]{:S(2)}, u32[]{:S(2)}) async-start(bf16[4,4,32,128]{3,2,1,0:T(8,128)(2,1)} %broadcast_select_fusion), calls=%async_computation | async-start | bytes 262144 | tf_op jit(solution)/shard_map/all_to_all | solution.py:25
  8.1 1.0 %compare_and_fusion.4 = (pred[64]{0:T(512)(128)(4,1)S(1)}, s32[64]{0:T(128)S(1)}, pred[64]{0:T(512)(128)(4,1)S(1)}, s32[64]{0:T(128)S(1)}, pred[64]{0:T(512)(128...) fusion(s32[64,16]{0,1:T(8,128)} %param.11), kind=kLoop, calls=%fused_computation.191 | loop fusion | flops 6144 | bytes 9216 | tf_op jit(solution)/shard_map/jit(_take)/and | solution.py:9
  9.2 0.7 broadcast_compare_fusion.4
  10.0 3.2 %all-to-all-done = bf16[4,4,32,128]{3,2,1,0:T(8,128)(2,1)S(1)} async-done(((bf16[4,4,32,128]{3,2,1,0:T(8,128)(2,1)}), bf16[4,4,32,128]{3,2,1,0:T(8,128)(2,1)S(1)}, u32[]{:S(2)}, u32[]{:S(2)}) %all-to-all-start) | async-done | bytes 131104 | tf_op jit(solution)/shard_map/all_to_all | solution.py:25
  13.2 0.1 pad_maximum_fusion
  13.2 1.5 %gather_fusion.2 = bf16[64,32,128]{2,1,0:T(8,128)(2,1)} fusion(bf16[80,32,128]{2,1,0:T(8,128)(2,1)S(1)} %pad_maximum_fusion, s32[1024]{0:T(1024)S(1)} %get-tuple-element.98), kind=kCustom, calls=%fused_computation.1.clone | custom fusion | bytes 1048832 | tf_op jit(solution)/shard_map/jit(_take)/gather | solution.py:9
  14.7 1.4 %gather_fusion.3 = bf16[64,32,128]{2,1,0:T(8,128)(2,1)} fusion(bf16[80,32,128]{2,1,0:T(8,128)(2,1)S(1)} %pad_maximum_fusion, s32[1024]{0:T(1024)S(1)} %get-tuple-element.97), kind=kCustom, calls=%fused_computation.2.clone | custom fusion | bytes 1048832 | tf_op jit(solution)/shard_map/jit(_take)/gather | solution.py:9
  16.1 1.4 %gather_fusion.4 = bf16[64,32,128]{2,1,0:T(8,128)(2,1)} fusion(bf16[80,32,128]{2,1,0:T(8,128)(2,1)S(1)} %pad_maximum_fusion, s32[1024]{0:T(1024)S(1)} %get-tuple-element.96), kind=kCustom, calls=%fused_computation.3.clone | custom fusion | bytes 1048832 | tf_op jit(solution)/shard_map/jit(_take)/gather | solution.py:9
  17.5 1.4 %gather_fusion.5 = bf16[64,32,128]{2,1,0:T(8,128)(2,1)} fusion(bf16[80,32,128]{2,1,0:T(8,128)(2,1)S(1)} %pad_maximum_fusion, s32[1024]{0:T(1024)S(1)} %get-tuple-element.95), kind=kCustom, calls=%fused_computation.4.clone | custom fusion | bytes 1048832 | tf_op jit(solution)/shard_map/jit(_take)/gather | solution.py:9
  19.0 1.4 %gather_fusion.6 = bf16[64,32,128]{2,1,0:T(8,128)(2,1)} fusion(bf16[80,32,128]{2,1,0:T(8,128)(2,1)S(1)} %pad_maximum_fusion, s32[1024]{0:T(1024)S(1)} %get-tuple-element.94), kind=kCustom, calls=%fused_computation.5.clone | custom fusion | bytes 1048832 | tf_op jit(solution)/shard_map/jit(_take)/gather | solution.py:9
  20.4 0.7 gather_fusion.1
  21.0 1.4 %gather_fusion.9 = bf16[64,32,128]{2,1,0:T(8,128)(2,1)} fusion(bf16[80,32,128]{2,1,0:T(8,128)(2,1)S(1)} %pad_maximum_fusion, s32[1024]{0:T(1024)S(1)} %get-tuple-element.91), kind=kCustom, calls=%fused_computation.8.clone | custom fusion | bytes 1048832 | tf_op jit(solution)/shard_map/jit(_take)/gather | solution.py:9
  22.5 1.4 %gather_fusion.10 = bf16[64,32,128]{2,1,0:T(8,128)(2,1)} fusion(bf16[80,32,128]{2,1,0:T(8,128)(2,1)S(1)} %pad_maximum_fusion, s32[1024]{0:T(1024)S(1)} %get-tuple-element.90), kind=kCustom, calls=%fused_computation.9.clone | custom fusion | bytes 1048832 | tf_op jit(solution)/shard_map/jit(_take)/gather | solution.py:9
  23.9 1.4 %gather_fusion.11 = bf16[64,32,128]{2,1,0:T(8,128)(2,1)} fusion(bf16[80,32,128]{2,1,0:T(8,128)(2,1)S(1)} %pad_maximum_fusion, s32[1024]{0:T(1024)S(1)} %get-tuple-element.89), kind=kCustom, calls=%fused_computation.10.clone | custom fusion | bytes 1048832 | tf_op jit(solution)/shard_map/jit(_take)/gather | solution.py:9
  25.4 1.4 %gather_fusion.8 = bf16[64,32,128]{2,1,0:T(8,128)(2,1)} fusion(bf16[80,32,128]{2,1,0:T(8,128)(2,1)S(1)} %pad_maximum_fusion, s32[1024]{0:T(1024)S(1)} %get-tuple-element.92), kind=kCustom, calls=%fused_computation.7.clone | custom fusion | bytes 1048832 | tf_op jit(solution)/shard_map/jit(_take)/gather | solution.py:9
  26.8 0.7 gather_fusion.7
  27.5 1.4 %gather_fusion.13 = bf16[64,32,128]{2,1,0:T(8,128)(2,1)} fusion(bf16[80,32,128]{2,1,0:T(8,128)(2,1)S(1)} %pad_maximum_fusion, s32[1024]{0:T(1024)S(1)} %get-tuple-element.87), kind=kCustom, calls=%fused_computation.12.clone | custom fusion | bytes 1048832 | tf_op jit(solution)/shard_map/jit(_take)/gather | solution.py:9
  28.9 1.4 %gather_fusion.14 = bf16[64,32,128]{2,1,0:T(8,128)(2,1)} fusion(bf16[80,32,128]{2,1,0:T(8,128)(2,1)S(1)} %pad_maximum_fusion, s32[1024]{0:T(1024)S(1)} %get-tuple-element.86), kind=kCustom, calls=%fused_computation.13.clone | custom fusion | bytes 1048832 | tf_op jit(solution)/shard_map/jit(_take)/gather | solution.py:9
  30.3 1.4 %gather_fusion.15 = bf16[64,32,128]{2,1,0:T(8,128)(2,1)} fusion(bf16[80,32,128]{2,1,0:T(8,128)(2,1)S(1)} %pad_maximum_fusion, s32[1024]{0:T(1024)S(1)} %get-tuple-element.85), kind=kCustom, calls=%fused_computation.14.clone | custom fusion | bytes 1048832 | tf_op jit(solution)/shard_map/jit(_take)/gather | solution.py:9
  31.7 0.7 gather_fusion.16
  32.4 0.7 gather_fusion.12
  33.0 0.0 copy-start.2
  33.0 0.0 copy-start.1
  33.1 3.1 %fusion.66 = f32[64,32,128]{2,1,0:T(8,128)S(1)} fusion(bf16[64,16,128,128]{3,2,1,0:T(8,128)(2,1)} %param.10, bf16[64,32,128]{2,1,0:T(8,128)(2,1)} %gather_fusion.2, pred[64]{0:T(512)(128)(4,1)S(1)} %get-tuple-element.60, pred[64]{0:T(512)(128)(4,1)S(1)} %get-tuple-element.80), kind=kOutput, calls=%fused_computation.71 | convolution fusion | flops 67633152 | bytes 3670144 | tf_op jit(solution)/shard_map/rcj,rij->cri/dot_general | solution.py:11
  36.1 3.0 %fusion.69 = f32[64,32,128]{2,1,0:T(8,128)S(1)} fusion(bf16[64,16,128,128]{3,2,1,0:T(8,128)(2,1)} %param.10, bf16[64,32,128]{2,1,0:T(8,128)(2,1)} %gather_fusion.3, pred[64]{0:T(512)(128)(4,1)S(1)} %get-tuple-element.58, pred[64]{0:T(512)(128)(4,1)S(1)} %get-tuple-element.79), kind=kOutput, calls=%fused_computation.72 | convolution fusion | flops 67633152 | bytes 3670144 | tf_op jit(solution)/shard_map/rcj,rij->cri/dot_general | solution.py:11
  39.2 3.0 %fusion.72 = f32[64,32,128]{2,1,0:T(8,128)S(1)} fusion(bf16[64,16,128,128]{3,2,1,0:T(8,128)(2,1)} %param.10, bf16[64,32,128]{2,1,0:T(8,128)(2,1)} %gather_fusion.4, pred[64]{0:T(512)(128)(4,1)S(1)} %get-tuple-element.56, pred[64]{0:T(512)(128)(4,1)S(1)} %get-tuple-element.78), kind=kOutput, calls=%fused_computation.73 | convolution fusion | flops 67633152 | bytes 3670144 | tf_op jit(solution)/shard_map/rcj,rij->cri/dot_general | solution.py:11
  42.2 0.0 copy-start.3
  42.2 0.0 copy-start.4
  42.2 3.0 %fusion.75 = f32[64,32,128]{2,1,0:T(8,128)S(1)} fusion(bf16[64,16,128,128]{3,2,1,0:T(8,128)(2,1)} %param.10, bf16[64,32,128]{2,1,0:T(8,128)(2,1)} %gather_fusion.5, pred[64]{0:T(512)(128)(4,1)S(1)} %get-tuple-element.54, pred[64]{0:T(512)(128)(4,1)S(1)} %get-tuple-element.77), kind=kOutput, calls=%fused_computation.74 | convolution fusion | flops 67633152 | bytes 3670144 | tf_op jit(solution)/shard_map/rcj,rij->cri/dot_general | solution.py:11
  45.2 3.0 %fusion.78 = f32[64,32,128]{2,1,0:T(8,128)S(1)} fusion(bf16[64,16,128,128]{3,2,1,0:T(8,128)(2,1)} %param.10, bf16[64,32,128]{2,1,0:T(8,128)(2,1)} %gather_fusion.6, pred[64]{0:T(512)(128)(4,1)S(1)} %get-tuple-element.52, pred[64]{0:T(512)(128)(4,1)S(1)} %get-tuple-element.76), kind=kOutput, calls=%fused_computation.75 | convolution fusion | flops 67633152 | bytes 3670144 | tf_op jit(solution)/shard_map/rcj,rij->cri/dot_general | solution.py:11
  48.3 3.0 %fusion.102 = f32[64,32,128]{2,1,0:T(8,128)S(1)} fusion(bf16[64,16,128,128]{3,2,1,0:T(8,128)(2,1)} %param.10, bf16[64,32,128]{2,1,0:T(8,128)(2,1)} %gather_fusion.9, pred[64]{0:T(512)(128)(4,1)S(1)} %get-tuple-element.46, pred[64]{0:T(512)(128)(4,1)S(1)} %get-tuple-element.73), kind=kOutput, calls=%fused_computation.83 | convolution fusion | flops 67633152 | bytes 3670144 | tf_op jit(solution)/shard_map/rcj,rij->cri/dot_general | solution.py:11
  51.3 3.0 %fusion.105 = f32[64,32,128]{2,1,0:T(8,128)S(1)} fusion(bf16[64,16,128,128]{3,2,1,0:T(8,128)(2,1)} %param.10, bf16[64,32,128]{2,1,0:T(8,128)(2,1)} %gather_fusion.10, pred[64]{0:T(512)(128)(4,1)S(1)} %get-tuple-element.44, pred[64]{0:T(512)(128)(4,1)S(1)} %get-tuple-element.72), kind=kOutput, calls=%fused_computation.84 | convolution fusion | flops 67633152 | bytes 3670144 | tf_op jit(solution)/shard_map/rcj,rij->cri/dot_general | solution.py:11
  54.3 3.0 %fusion.108 = f32[64,32,128]{2,1,0:T(8,128)S(1)} fusion(bf16[64,16,128,128]{3,2,1,0:T(8,128)(2,1)} %param.10, bf16[64,32,128]{2,1,0:T(8,128)(2,1)} %gather_fusion.11, pred[64]{0:T(512)(128)(4,1)S(1)} %get-tuple-element.42, pred[64]{0:T(512)(128)(4,1)S(1)} %get-tuple-element.71), kind=kOutput, calls=%fused_computation.85 | convolution fusion | flops 67633152 | bytes 3670144 | tf_op jit(solution)/shard_map/rcj,rij->cri/dot_general | solution.py:11
  57.3 3.0 %fusion.99 = f32[64,32,128]{2,1,0:T(8,128)S(1)} fusion(bf16[64,16,128,128]{3,2,1,0:T(8,128)(2,1)} %param.10, bf16[64,32,128]{2,1,0:T(8,128)(2,1)} %gather_fusion.8, pred[64]{0:T(512)(128)(4,1)S(1)} %get-tuple-element.48, pred[64]{0:T(512)(128)(4,1)S(1)} %get-tuple-element.74), kind=kOutput, calls=%fused_computation.82 | convolution fusion | flops 67633152 | bytes 3670144 | tf_op jit(solution)/shard_map/rcj,rij->cri/dot_general | solution.py:11
  60.4 3.0 %fusion.132 = f32[64,32,128]{2,1,0:T(8,128)S(1)} fusion(bf16[64,16,128,128]{3,2,1,0:T(8,128)(2,1)} %param.10, bf16[64,32,128]{2,1,0:T(8,128)(2,1)} %gather_fusion.13, pred[64]{0:T(512)(128)(4,1)S(1)} %get-tuple-element.40, pred[64]{0:T(512)(128)(4,1)S(1)} %get-tuple-element.70), kind=kOutput, calls=%fused_computation.93 | convolution fusion | flops 67633152 | bytes 3670144 | tf_op jit(solution)/shard_map/rcj,rij->cri/dot_general | solution.py:11
  63.4 0.0 copy-done.2
  63.4 2.9 %fusion.135 = f32[64,32,128]{2,1,0:T(8,128)S(1)} fusion(bf16[64,16,128,128]{3,2,1,0:T(8,128)(2,1)} %param.10, bf16[64,32,128]{2,1,0:T(8,128)(2,1)S(1)} %copy-done.2, pred[64]{0:T(512)(128)(4,1)S(1)} %get-tuple-element.38, pred[64]{0:T(512)(128)(4,1)S(1)} %get-tuple-element.69), kind=kOutput, calls=%fused_computation.94 | convolution fusion | flops 67633152 | bytes 3670144 | tf_op jit(solution)/shard_map/rcj,rij->cri/dot_general | solution.py:11
  66.2 0.0 copy-done.1
  66.2 2.9 %fusion.138 = f32[64,32,128]{2,1,0:T(8,128)S(1)} fusion(bf16[64,16,128,128]{3,2,1,0:T(8,128)(2,1)} %param.10, bf16[64,32,128]{2,1,0:T(8,128)(2,1)S(1)} %copy-done.1, pred[64]{0:T(512)(128)(4,1)S(1)} %get-tuple-element.66, pred[64]{0:T(512)(128)(4,1)S(1)} %get-tuple-element.83), kind=kOutput, calls=%fused_computation.95 | convolution fusion | flops 67633152 | bytes 3670144 | tf_op jit(solution)/shard_map/rcj,rij->cri/dot_general | solution.py:11
  69.1 3.0 %fusion.141 = f32[64,32,128]{2,1,0:T(8,128)S(1)} fusion(bf16[64,16,128,128]{3,2,1,0:T(8,128)(2,1)} %param.10, bf16[64,32,128]{2,1,0:T(8,128)(2,1)S(1)} %gather_fusion.16, pred[64]{0:T(512)(128)(4,1)S(1)} %get-tuple-element.64, pred[64]{0:T(512)(128)(4,1)S(1)} %get-tuple-element.82), kind=kOutput, calls=%fused_computation.96 | convolution fusion | flops 67633152 | bytes 3670144 | tf_op jit(solution)/shard_map/rcj,rij->cri/dot_general | solution.py:11
  72.1 2.9 %fusion.63 = f32[64,32,128]{2,1,0:T(8,128)S(1)} fusion(f32[64,32,128]{2,1,0:T(8,128)S(1)} %fusion.78, f32[64,32,128]{2,1,0:T(8,128)S(1)} %fusion.75, f32[64,32,128]{2,1,0:T(8,128)S(1)} %fusion.72, f32[64,32,128]{2,1,0:T(8,128)S(1)} %fusion.69, f32[64,32,128]{2,1,0:T(8,128)S(1)} %fusion.66, bf16[64,16,128,128]{3,2,1,0:T(8,128)(2,1)} %param.10, ...), kind=kOutput, calls=%fused_computation.70 | convolution fusion | flops 68943872 | bytes 8913024 | tf_op jit(solution)/shard_map/rcj,rij->cri/dot_general | solution.py:11
  75.0 2.9 %fusion.96 = f32[64,32,128]{2,1,0:T(8,128)S(1)} fusion(f32[64,32,128]{2,1,0:T(8,128)S(1)} %fusion.108, f32[64,32,128]{2,1,0:T(8,128)S(1)} %fusion.105, f32[64,32,128]{2,1,0:T(8,128)S(1)} %fusion.102, f32[64,32,128]{2,1,0:T(8,128)S(1)} %fusion.99, f32[64,32,128]{2,1,0:T(8,128)S(1)} %fusion.63, bf16[64,16,128,128]{3,2,1,0:T(8,128)(2,1)} %param.10, ...), kind=kOutput, calls=%fused_computation.81 | convolution fusion | flops 68943872 | bytes 8913024 | tf_op jit(solution)/shard_map/rcj,rij->cri/dot_general | solution.py:11
  78.0 2.9 %fusion.146 = bf16[32,64,128]{2,0,1:T(8,128)(2,1)S(1)} fusion(f32[64,32,128]{2,1,0:T(8,128)S(1)} %fusion.141, f32[64,32,128]{2,1,0:T(8,128)S(1)} %fusion.138, f32[64,32,128]{2,1,0:T(8,128)S(1)} %fusion.135, f32[64,32,128]{2,1,0:T(8,128)S(1)} %fusion.132, f32[64,32,128]{2,1,0:T(8,128)S(1)} %fusion.96, bf16[64,16,128,128]{3,2,1,0:T(8,128)(2,1)} %param.10, ...), kind=kOutput, calls=%fused_computation.100 | convolution fusion | flops 69206016 | bytes 8388736 | tf_op jit(solution)/shard_map/rcj,rij->cri/dot_general | solution.py:11
  80.9 0.2 copy.78
  81.1 0.2 all_to_all.18
  81.3 0.3 copy.79
  81.6 20.0 %all_to_all.24 = bf16[32,8,1024]{2,0,1:T(8,128)(2,1)S(1)} all-to-all(bf16[32,8,1024]{2,0,1:T(8,128)(2,1)S(1)} %copy.79), channel_id=1, replica_groups=mesh['vert'=4,'feat'=8] {'feat'}, dimensions={1} | all-to-all | bytes 1048576 | tf_op jit(solution)/shard_map/all_to_all | solution.py:33
  101.6 0.0 copy-done.3
  101.6 0.0 copy-done.4
  101.6 1.2 %fusion.145 = bf16[1024,256]{1,0:T(8,128)(2,1)} fusion(bf16[256,1024]{1,0:T(8,128)(2,1)S(1)} %bitcast.221, bf16[256,256]{1,0:T(8,128)(2,1)S(1)} %copy-done.3, f32[256]{0:T(256)S(1)} %copy-done.4), kind=kOutput, calls=%fused_computation.99 | convolution fusion | flops 135004160 | bytes 1180672 | tf_op jit(solution)/shard_map/dot_general | solution.py:34
  (9 shorter events, 0.1 us)
Async XLA Ops:
  0.0 1.4 %copy-start = (bf16[8192,32]{0,1:T(8,128)(2,1)S(1)}, bf16[8192,32]{0,1:T(8,128)(2,1)}, u32[]{:S(2)}) copy-start(bf16[8192,32]{0,1:T(8,128)(2,1)} %param.9) | copy-start | bytes 1572868
  2.9 10.2 %all-to-all-start = ((bf16[4,4,32,128]{3,2,1,0:T(8,128)(2,1)}), bf16[4,4,32,128]{3,2,1,0:T(8,128)(2,1)S(1)}, u32[]{:S(2)}, u32[]{:S(2)}) async-start(bf16[4,4,32,128]{3,2,1,0:T(8,128)(2,1)} %broadcast_select_fusion), calls=%async_computation | async-start | bytes 262144 | tf_op jit(solution)/shard_map/all_to_all | solution.py:25
  33.0 30.4 %copy-start.2 = (bf16[64,32,128]{2,1,0:T(8,128)(2,1)S(1)}, bf16[64,32,128]{2,1,0:T(8,128)(2,1)}, u32[]{:S(2)}) copy-start(bf16[64,32,128]{2,1,0:T(8,128)(2,1)} %gather_fusion.14) | copy-start | bytes 1572868
  33.0 33.2 %copy-start.1 = (bf16[64,32,128]{2,1,0:T(8,128)(2,1)S(1)}, bf16[64,32,128]{2,1,0:T(8,128)(2,1)}, u32[]{:S(2)}) copy-start(bf16[64,32,128]{2,1,0:T(8,128)(2,1)} %gather_fusion.15) | copy-start | bytes 1572868
  42.2 59.5 %copy-start.3 = (bf16[256,256]{1,0:T(8,128)(2,1)S(1)}, bf16[256,256]{1,0:T(8,128)(2,1)}, u32[]{:S(2)}) copy-start(bf16[256,256]{1,0:T(8,128)(2,1)} %param.14) | copy-start | bytes 393220
  42.2 59.5 %copy-start.4 = (f32[256]{0:T(256)S(1)}, f32[256]{0:T(256)}, u32[]{:S(2)}) copy-start(f32[256]{0:T(256)} %param.15) | copy-start | bytes 3076
where the time goes:
time: 104 us; the launch traced here: 103 us
  matrix products  48.9 us (47%)
  local copies, waits for them, and re-layouts  21.3 us (20%)
  blocking collectives  20 us (19%)
  starting transfers between devices  5.19 us (5%)
  other arithmetic  4.01 us (4%)
  waiting for transfers between devices  3.18 us (3%)
    dot_general x16, matrix products, add_tile(): jnp.einsum('rcj,rij->cri', picked, tile_page, preferred_element_type=jnp....  47.8 us
    all_to_all x1, blocking collectives, per_device(): lax.all_to_all(hidden, 'feat', split_axis=1, concat_axis=0, tiled=True)  20 us
    gather x16, local copies, waits for them, and re-layouts, add_tile(): picked = jnp.take(extended, wanted, axis=0)  19.8 us
    all_to_all x1, starting transfers between devices, per_device(): lax.all_to_all(chosen, 'vert', split_axis=0, concat_axis=0, tiled=True)  5.19 us
    all_to_all x1, waiting for transfers between devices, per_device(): lax.all_to_all(chosen, 'vert', split_axis=0, concat_axis=0, tiled=True)  3.18 us
  transfers between devices with their start and end apart: 1, of which 1 were waited for; matrix products, arithmetic and copies ran while one was open for 2% of the time, Pallas kernels for 0%

commit v1 on v0

v1 whole, which is shorter than its diff:
```python
import functools

import jax
import jax.numpy as jnp
from jax import lax
from jax.experimental import pallas as pl
from jax.experimental.pallas import tpu as pltpu
from jax.sharding import PartitionSpec as P

MESH = pl.DeviceIdType.MESH
GROUP = 4
WINDOW = 6


def flipped(index, mask, count):
    total = 0
    bit = 1
    while bit < count:
        total = total + bit * ((index // bit + mask // bit) % 2)
        bit *= 2
    return total


def exchange_kernel(
    dims, cols, send, features, tiles, gathered,
    extended, local, outgoing, hidden, pages,
    load_sem, page_sem, halo_send, halo_recv, full_send, full_recv,
):
    verts, feats, blocks, depth, edge, width, slots, group, window = dims
    per_dest = blocks // feats
    parts = per_dest // group
    chunks = feats * parts
    span = group * edge
    vert = lax.axis_index("vert")
    feat = lax.axis_index("feat")

    def dest_of(chunk):
        return flipped(feat, feats - 1 - chunk // parts, feats)

    def page_copy(chunk):
        first = dest_of(chunk) * per_dest + (chunk % parts) * group
        slot = chunk % window
        return pltpu.make_async_copy(
            tiles.at[pl.ds(first, group)], pages.at[slot], page_sem.at[slot]
        )

    local_copy = pltpu.make_async_copy(features, local, load_sem)
    local_copy.start()
    for chunk in range(window):
        page_copy(chunk).start()
    extended[blocks + verts * slots] = jnp.zeros((width, edge), jnp.bfloat16)
    local_copy.wait()
    for block in range(blocks):
        extended[block] = local[:, pl.ds(block * edge, edge)]
    for step in range(verts):
        peer = (vert + step) % verts
        for slot in range(slots):
            outgoing[step, slot] = extended[send[peer * slots + slot]]
    barrier = pltpu.get_barrier_semaphore()
    for step in range(1, verts):
        pl.semaphore_signal(
            barrier, inc=1, device_id=((vert + step) % verts, feat), device_id_type=MESH
        )
    for step in range(1, feats):
        pl.semaphore_signal(
            barrier, inc=1, device_id=(vert, (feat + step) % feats), device_id_type=MESH
        )
    own_halo = pl.ds(blocks + vert * slots, slots)
    pl.semaphore_wait(barrier, verts + feats - 2)
    halos = []
    for step in range(1, verts):
        halo = pltpu.make_async_remote_copy(
            src_ref=outgoing.at[step],
            dst_ref=extended.at[own_halo],
            send_sem=halo_send.at[step],
            recv_sem=halo_recv.at[step],
            device_id=((vert + step) % verts, feat),
            device_id_type=MESH,
        )
        halo.start()
        halos.append(halo)
    extended[own_halo] = outgoing[0]
    for halo in halos:
        halo.wait()

    def outputs_of(chunk):
        at = pl.multiple_of((chunk % parts) * span, edge)
        return (
            hidden.at[chunk // parts, :, pl.ds(at, span)],
            gathered.at[pl.ds(pl.multiple_of(feat * width, width), width), pl.ds(at, span)],
        )

    def full_copy(chunk):
        source, target = outputs_of(chunk)
        return pltpu.make_async_remote_copy(
            src_ref=source,
            dst_ref=target,
            send_sem=full_send.at[chunk],
            recv_sem=full_recv.at[chunk],
            device_id=(vert, dest_of(chunk)),
            device_id_type=MESH,
        )

    def aggregate(chunk, carry):
        page_copy(chunk).wait()
        slot = chunk % window
        first = dest_of(chunk) * per_dest + (chunk % parts) * group
        for row in range(group):
            picked = []
            for place in range(depth):
                picked.append(extended[cols[(first + row) * depth + place]])
            page = jnp.concatenate([pages[slot, row, place] for place in range(depth)], axis=1)
            total = lax.dot_general(
                page,
                jnp.concatenate(picked, axis=1),
                (((1,), (1,)), ((), ())),
                preferred_element_type=jnp.float32,
            )
            at = pl.multiple_of((chunk % parts) * span + row * edge, edge)
            hidden[chunk // parts, :, pl.ds(at, edge)] = total.T.astype(jnp.bfloat16)

        @pl.when(chunk + window < chunks)
        def _():
            page_copy(chunk + window).start()

        @pl.when(chunk < chunks - parts)
        def _():
            full_copy(chunk).start()

        return carry

    lax.fori_loop(0, chunks, aggregate, 0)
    gathered[pl.ds(pl.multiple_of(feat * width, width), width), :] = hidden[feats - 1]

    def finish(chunk, carry):
        full_copy(chunk).wait()
        return carry

    lax.fori_loop(0, chunks - parts, finish, 0)


def per_device(features, tiles, tile_cols, tile_count, send_list, weight, bias):
    blocks, depth, edge = tiles.shape[:3]
    width = features.shape[1]
    verts, feats = lax.axis_size("vert"), lax.axis_size("feat")
    slots = send_list.shape[2]
    per_dest = blocks // feats
    group = min(GROUP, per_dest)
    chunks = blocks // group
    window = min(WINDOW, chunks)
    rows = per_dest * edge
    dead = blocks + verts * slots
    is_live = jnp.arange(depth, dtype=jnp.int32)[None, :] < tile_count[:, None]
    cols = jnp.where(is_live, tile_cols, dead).reshape(-1)
    dims = (verts, feats, blocks, depth, edge, width, slots, group, window)
    gathered = pl.pallas_call(
        functools.partial(exchange_kernel, dims),
        out_shape=jax.ShapeDtypeStruct((feats * width, rows), jnp.bfloat16),
        in_specs=[
            pl.BlockSpec(memory_space=pltpu.SMEM),
            pl.BlockSpec(memory_space=pltpu.SMEM),
            pl.BlockSpec(memory_space=pl.ANY),
            pl.BlockSpec(memory_space=pl.ANY),
        ],
        out_specs=pl.BlockSpec(memory_space=pltpu.VMEM),
        scratch_shapes=[
            pltpu.VMEM((dead + 1, width, edge), jnp.bfloat16),
            pltpu.VMEM((width, blocks * edge), jnp.bfloat16),
            pltpu.VMEM((verts, slots, width, edge), jnp.bfloat16),
            pltpu.VMEM((feats, width, rows), jnp.bfloat16),
            pltpu.VMEM((window, group, depth, edge, edge), jnp.bfloat16),
            pltpu.SemaphoreType.DMA,
            pltpu.SemaphoreType.DMA((window,)),
            pltpu.SemaphoreType.DMA((verts,)),
            pltpu.SemaphoreType.DMA((verts,)),
            pltpu.SemaphoreType.DMA((chunks,)),
            pltpu.SemaphoreType.DMA((chunks,)),
        ],
        compiler_params=pltpu.CompilerParams(
            collective_id=0, has_side_effects=True, vmem_limit_bytes=60 * 1024 * 1024
        ),
    )(cols, send_list.reshape(-1), features.T, tiles)
    mixed_rows = lax.dot_general(
        gathered, weight, (((0,), (0,)), ((), ())), preferred_element_type=jnp.float32
    )
    return jnp.maximum(mixed_rows + bias, jnp.float32(0.0)).astype(jnp.bfloat16)


def solution(mesh):
    return jax.shard_map(
        per_device,
        mesh=mesh,
        in_specs=(
            P("vert", "feat"),
            P("vert", None, None, None),
            P("vert", None),
            P("vert"),
            P("vert", None, None),
            P(),
            P(),
        ),
        out_specs=P(("vert", "feat"), None),
        check_vma=False,
    )
```

time: 104 us -> 34.6 us (0.33)
  matrix products: 48.9 us -> 2.19 us
  Pallas kernels: 0 us -> 29.3 us
  blocking collectives: 20 us -> 0 us
  local copies, waits for them, and re-layouts: 21.3 us -> 2.14 us
  starting transfers between devices: 5.19 us -> 0 us
  other arithmetic: 4.01 us -> 0.7 us
  waiting for transfers between devices: 3.18 us -> 0 us
    dot_general x17 -> x1, matrix products: 48.9 us -> 2.19 us  [per_device(): lax.dot_general(gathered, weight, (((0,), (0,)), ((), ())), preferred_ele...]
    pallas_call x0 -> x1, Pallas kernels: none -> 29.3 us  [per_device(): pl.pallas_call(functools.partial(exchange_kernel, dims), out_shape=jax.Sh...]
    gather x17 -> x0, local copies, waits for them, and re-layouts: 20.4 us -> none  [the longest x16 19.8 us: add_tile(): picked = jnp.take(extended, wanted, axis=0)]
    all_to_all x1 -> x0, blocking collectives: 20 us -> none  [per_device(): lax.all_to_all(hidden, 'feat', split_axis=1, concat_axis=0, tiled=True)]
    all_to_all x1 -> x0, starting transfers between devices: 5.19 us -> none  [per_device(): lax.all_to_all(chosen, 'vert', split_axis=0, concat_axis=0, tiled=True)]
    all_to_all x1 -> x0, waiting for transfers between devices: 3.18 us -> none  [per_device(): lax.all_to_all(chosen, 'vert', split_axis=0, concat_axis=0, tiled=True)]
    reshape x0 -> x2, local copies, waits for them, and re-layouts: none -> 2.05 us  [the longest x1 1.38 us: per_device(): send_list.reshape(-1)]
    and x2 -> x0, other arithmetic: 1.73 us -> none  [the longest x1 1.05 us: add_tile(): picked = jnp.take(extended, wanted, axis=0)]
  transfers between devices with their start and end apart: 1 -> 0, of which waited for: 1 -> 0; matrix products, arithmetic and copies ran while one was open for 2% -> 0% of each run, Pallas kernels for 0% -> 0%
where the time goes in v1:
time: 34.6 us; the launch traced here: 34.4 us
  Pallas kernels  29.3 us (85%)
  matrix products  2.19 us (6%)
  local copies, waits for them, and re-layouts  2.14 us (6%)
  other arithmetic  0.7 us (2%)
    pallas_call x1, Pallas kernels, per_device(): pl.pallas_call(functools.partial(exchange_kernel, dims), out_shape=jax.Sh...  29.3 us
    dot_general x1, matrix products, per_device(): lax.dot_general(gathered, weight, (((0,), (0,)), ((), ())), preferred_ele...  2.19 us
    reshape x1, local copies, waits for them, and re-layouts, per_device(): send_list.reshape(-1)  1.38 us
    select_n x1, other arithmetic, per_device(): cols = jnp.where(is_live, tile_cols, dead).reshape(-1)  0.7 us

profile of v1, /device:TPU:0, one launch (start us, length us, event | category | flops | bytes accessed | tf_op | source)
XLA Modules:
  0.0 34.4 jit_solution(16117104188442978333)
XLA Ops:
  0.0 0.0 copy-start
  0.0 0.0 copy-start.1
  0.0 1.4 %reshape.9.send = s32[16]{0:T(128)} reshape(s32[1,4,4]{2,1,0:T(4,128)} %param.11) | data formatting | bytes 128 | tf_op jit(solution)/shard_map/reshape | solution.py:182
  1.4 0.7 %fusion.2 = s32[64,16]{0,1:T(8,128)S(1)} fusion(s32[64,16]{0,1:T(8,128)} %param.9, s32[64]{0:T(128)} %param.10), kind=kLoop, calls=%fused_computation.4 | loop fusion | flops 2048 | bytes 8448 | tf_op jit(solution)/shard_map/jit(_where)/select_n | solution.py:154
  2.1 0.1 copy.8
  2.2 0.7 %reshape.8.cols = s32[1024]{0:T(1024)} reshape(s32[64,16]{1,0:T(8,128)S(1)} %copy.8) | data formatting | bytes 8192 | tf_op jit(solution)/shard_map/reshape | solution.py:154
  2.8 29.3 %shard_map.73 = bf16[256,1024]{1,0:T(8,128)(2,1)} custom-call(s32[1024]{0:T(1024)} %reshape.8.cols, s32[16]{0:T(128)} %reshape.9.send, bf16[32,8192]{1,0:T(8,128)(2,1)} %bitcast.3, bf16[64,16,128,128]{3,2,1,0:T(8,128)(2,1)} %tiles.1), custom_call_target="tpu_custom_call" | custom-call | tf_op jit(solution)/shard_map/pallas_call | solution.py:156
  32.2 0.0 copy-done
  32.2 0.0 copy-done.1
  32.2 2.2 %fusion.1 = bf16[1024,256]{1,0:T(8,128)(2,1)} fusion(bf16[256,1024]{1,0:T(8,128)(2,1)} %shard_map.73, bf16[256,256]{1,0:T(8,128)(2,1)S(1)} %copy-done, f32[256]{0:T(256)S(1)} %copy-done.1), kind=kOutput, calls=%fused_computation.2 | convolution fusion | flops 135004160 | bytes 1180672 | tf_op jit(solution)/shard_map/dot_general | solution.py:183
Async XLA Ops:
  0.0 32.2 %copy-start = (bf16[256,256]{1,0:T(8,128)(2,1)S(1)}, bf16[256,256]{1,0:T(8,128)(2,1)}, u32[]{:S(2)}) copy-start(bf16[256,256]{1,0:T(8,128)(2,1)} %param.12) | copy-start | bytes 393220
  0.0 32.2 %copy-start.1 = (f32[256]{0:T(256)S(1)}, f32[256]{0:T(256)}, u32[]{:S(2)}) copy-start(f32[256]{0:T(256)} %param.13) | copy-start | bytes 3076

commit v2 on v1

--- a/solution.py
+++ b/solution.py
@@ -9,7 +9,7 @@
 
 MESH = pl.DeviceIdType.MESH
 GROUP = 4
-WINDOW = 6
+WINDOW = 16
 
 
 def flipped(index, mask, count):
@@ -22,8 +22,8 @@
 
 
 def exchange_kernel(
-    dims, cols, send, features, tiles, gathered,
-    extended, local, outgoing, hidden, pages,
+    dims, cols, count, send, features, tiles, gathered,
+    extended, local, outgoing, landed, hidden, pages,
     load_sem, page_sem, halo_send, halo_recv, full_send, full_recv,
 ):
     verts, feats, blocks, depth, edge, width, slots, group, window = dims
@@ -31,6 +31,7 @@
     parts = per_dest // group
     chunks = feats * parts
     span = group * edge
+    dead = blocks + verts * slots
     vert = lax.axis_index("vert")
     feat = lax.axis_index("feat")
 
@@ -46,32 +47,31 @@
 
     local_copy = pltpu.make_async_copy(features, local, load_sem)
     local_copy.start()
+    barrier = pltpu.get_barrier_semaphore()
+    for step in range(1, verts):
+        pl.semaphore_signal(
+            barrier, inc=1, device_id=((vert + step) % verts, feat), device_id_type=MESH
+        )
+    for step in range(1, feats):
+        pl.semaphore_signal(
+            barrier, inc=1, device_id=(vert, (feat + step) % feats), device_id_type=MESH
+        )
     for chunk in range(window):
         page_copy(chunk).start()
-    extended[blocks + verts * slots] = jnp.zeros((width, edge), jnp.bfloat16)
+    extended[dead] = jnp.zeros((width, edge), jnp.bfloat16)
     local_copy.wait()
     for block in range(blocks):
         extended[block] = local[:, pl.ds(block * edge, edge)]
     for step in range(verts):
         peer = (vert + step) % verts
         for slot in range(slots):
-            outgoing[step, slot] = extended[send[peer * slots + slot]]
-    barrier = pltpu.get_barrier_semaphore()
-    for step in range(1, verts):
-        pl.semaphore_signal(
-            barrier, inc=1, device_id=((vert + step) % verts, feat), device_id_type=MESH
-        )
-    for step in range(1, feats):
-        pl.semaphore_signal(
-            barrier, inc=1, device_id=(vert, (feat + step) % feats), device_id_type=MESH
-        )
-    own_halo = pl.ds(blocks + vert * slots, slots)
+            outgoing[step, slot] = extended[send[0, peer, slot]]
     pl.semaphore_wait(barrier, verts + feats - 2)
     halos = []
     for step in range(1, verts):
         halo = pltpu.make_async_remote_copy(
             src_ref=outgoing.at[step],
-            dst_ref=extended.at[own_halo],
+            dst_ref=landed.at[step],
             send_sem=halo_send.at[step],
             recv_sem=halo_recv.at[step],
             device_id=((vert + step) % verts, feat),
@@ -79,9 +79,11 @@
         )
         halo.start()
         halos.append(halo)
-    extended[own_halo] = outgoing[0]
-    for halo in halos:
-        halo.wait()
+    extended[pl.ds(blocks + vert * slots, slots)] = outgoing[0]
+    for step in range(1, verts):
+        halos[step - 1].wait()
+        source = (vert + verts - step) % verts
+        extended[pl.ds(blocks + source * slots, slots)] = landed[step]
 
     def outputs_of(chunk):
         at = pl.multiple_of((chunk % parts) * span, edge)
@@ -107,8 +109,10 @@
         first = dest_of(chunk) * per_dest + (chunk % parts) * group
         for row in range(group):
             picked = []
+            live = count[first + row]
             for place in range(depth):
-                picked.append(extended[cols[(first + row) * depth + place]])
+                column = jnp.where(place < live, cols[place, first + row], dead)
+                picked.append(extended[column])
             page = jnp.concatenate([pages[slot, row, place] for place in range(depth)], axis=1)
             total = lax.dot_general(
                 page,
@@ -150,13 +154,12 @@
     window = min(WINDOW, chunks)
     rows = per_dest * edge
     dead = blocks + verts * slots
-    is_live = jnp.arange(depth, dtype=jnp.int32)[None, :] < tile_count[:, None]
-    cols = jnp.where(is_live, tile_cols, dead).reshape(-1)
     dims = (verts, feats, blocks, depth, edge, width, slots, group, window)
     gathered = pl.pallas_call(
         functools.partial(exchange_kernel, dims),
         out_shape=jax.ShapeDtypeStruct((feats * width, rows), jnp.bfloat16),
         in_specs=[
+            pl.BlockSpec(memory_space=pltpu.SMEM),
             pl.BlockSpec(memory_space=pltpu.SMEM),
             pl.BlockSpec(memory_space=pltpu.SMEM),
             pl.BlockSpec(memory_space=pl.ANY),
@@ -166,6 +169,7 @@
         scratch_shapes=[
             pltpu.VMEM((dead + 1, width, edge), jnp.bfloat16),
             pltpu.VMEM((width, blocks * edge), jnp.bfloat16),
+            pltpu.VMEM((verts, slots, width, edge), jnp.bfloat16),
             pltpu.VMEM((verts, slots, width, edge), jnp.bfloat16),
             pltpu.VMEM((feats, width, rows), jnp.bfloat16),
             pltpu.VMEM((window, group, depth, edge, edge), jnp.bfloat16),
@@ -179,7 +183,7 @@
         compiler_params=pltpu.CompilerParams(
             collective_id=0, has_side_effects=True, vmem_limit_bytes=60 * 1024 * 1024
         ),
-    )(cols, send_list.reshape(-1), features.T, tiles)
+    )(tile_cols.T, tile_count, send_list, features.T, tiles)
     mixed_rows = lax.dot_general(
         gathered, weight, (((0,), (0,)), ((), ())), preferred_element_type=jnp.float32
     )

time: 34.6 us -> 27.8 us (0.80)
  Pallas kernels: 29.3 us -> 25.4 us
  local copies, waits for them, and re-layouts: 2.14 us -> 0.01 us
  other arithmetic: 0.7 us -> 0 us
    pallas_call x1, Pallas kernels: 29.3 us -> 25.4 us  [per_device(): pl.pallas_call(functools.partial(exchange_kernel, dims), out_shape=jax.Sh...]
    reshape x2 -> x0, local copies, waits for them, and re-layouts: 2.05 us -> none  [the longest x1 1.38 us: per_device(): send_list.reshape(-1)]
    select_n x1 -> x0, other arithmetic: 0.7 us -> none  [per_device(): cols = jnp.where(is_live, tile_cols, dead).reshape(-1)]
where the time goes in v2:
time: 27.8 us; the launch traced here: 27.7 us
  Pallas kernels  25.4 us (91%)
  matrix products  2.19 us (8%)
    pallas_call x1, Pallas kernels, per_device(): pl.pallas_call(functools.partial(exchange_kernel, dims), out_shape=jax.Sh...  25.4 us
    dot_general x1, matrix products, per_device(): lax.dot_general(gathered, weight, (((0,), (0,)), ((), ())), preferred_ele...  2.19 us

profile of v2, /device:TPU:0, one launch (start us, length us, event | category | flops | bytes accessed | tf_op | source)
XLA Modules:
  0.0 27.7 jit_solution(15615677154122751194)
XLA Ops:
  0.0 0.0 copy-start
  0.0 0.0 copy-start.1
  0.0 25.4 %shard_map.73 = bf16[256,1024]{1,0:T(8,128)(2,1)} custom-call(s32[16,64]{1,0:T(8,128)} %bitcast.5, s32[64]{0:T(128)} %count.1, s32[1,4,4]{2,1,0:T(4,128)} %send.1, bf16[32,8192]{1,0:T(8,128)(2,1)} %bitcast.4, bf16[64,16,128,128]{3,2,1,0:T(8,128)(2,1)} %tiles.1), custom_call_target="tpu_custom_call" | custom-call | tf_op jit(solution)/shard_map/pallas_call | solution.py:158
  25.4 0.0 copy-done
  25.4 0.0 copy-done.1
  25.5 2.2 %fusion.1 = bf16[1024,256]{1,0:T(8,128)(2,1)} fusion(bf16[256,1024]{1,0:T(8,128)(2,1)} %shard_map.73, bf16[256,256]{1,0:T(8,128)(2,1)S(1)} %copy-done, f32[256]{0:T(256)S(1)} %copy-done.1), kind=kOutput, calls=%fused_computation.2 | convolution fusion | flops 135004160 | bytes 1180672 | tf_op jit(solution)/shard_map/dot_general | solution.py:187
Async XLA Ops:
  0.0 25.4 %copy-start = (bf16[256,256]{1,0:T(8,128)(2,1)S(1)}, bf16[256,256]{1,0:T(8,128)(2,1)}, u32[]{:S(2)}) copy-start(bf16[256,256]{1,0:T(8,128)(2,1)} %param.12) | copy-start | bytes 393220
  0.0 25.4 %copy-start.1 = (f32[256]{0:T(256)S(1)}, f32[256]{0:T(256)}, u32[]{:S(2)}) copy-start(f32[256]{0:T(256)} %param.13) | copy-start | bytes 3076

commit v3 on v2

--- a/solution.py
+++ b/solution.py
@@ -22,8 +22,8 @@
 
 
 def exchange_kernel(
-    dims, cols, count, send, features, tiles, gathered,
-    extended, local, outgoing, landed, hidden, pages,
+    dims, cols_in, count_in, send_in, features, tiles, gathered,
+    cols, count, send, table_sem, extended, local, outgoing, landed, hidden, pages,
     load_sem, page_sem, halo_send, halo_recv, full_send, full_recv,
 ):
     verts, feats, blocks, depth, edge, width, slots, group, window = dims
@@ -47,6 +47,12 @@
 
     local_copy = pltpu.make_async_copy(features, local, load_sem)
     local_copy.start()
+    tables = [
+        pltpu.make_async_copy(source, target, table_sem.at[at])
+        for at, (source, target) in enumerate(((send_in, send), (cols_in, cols), (count_in, count)))
+    ]
+    for table in tables:
+        table.start()
     barrier = pltpu.get_barrier_semaphore()
     for step in range(1, verts):
         pl.semaphore_signal(
@@ -60,6 +66,8 @@
         page_copy(chunk).start()
     extended[dead] = jnp.zeros((width, edge), jnp.bfloat16)
     local_copy.wait()
+    for table in tables:
+        table.wait()
     for block in range(blocks):
         extended[block] = local[:, pl.ds(block * edge, edge)]
     for step in range(verts):
@@ -159,14 +167,18 @@
         functools.partial(exchange_kernel, dims),
         out_shape=jax.ShapeDtypeStruct((feats * width, rows), jnp.bfloat16),
         in_specs=[
-            pl.BlockSpec(memory_space=pltpu.SMEM),
-            pl.BlockSpec(memory_space=pltpu.SMEM),
-            pl.BlockSpec(memory_space=pltpu.SMEM),
-            pl.BlockSpec(memory_space=pl.ANY),
-            pl.BlockSpec(memory_space=pl.ANY),
+            pl.BlockSpec(memory_space=pltpu.HBM),
+            pl.BlockSpec(memory_space=pltpu.HBM),
+            pl.BlockSpec(memory_space=pltpu.HBM),
+            pl.BlockSpec(memory_space=pltpu.HBM),
+            pl.BlockSpec(memory_space=pltpu.HBM),
         ],
         out_specs=pl.BlockSpec(memory_space=pltpu.VMEM),
         scratch_shapes=[
+            pltpu.SMEM((depth, blocks), jnp.int32),
+            pltpu.SMEM((blocks,), jnp.int32),
+            pltpu.SMEM(send_list.shape, jnp.int32),
+            pltpu.SemaphoreType.DMA((3,)),
             pltpu.VMEM((dead + 1, width, edge), jnp.bfloat16),
             pltpu.VMEM((width, blocks * edge), jnp.bfloat16),
             pltpu.VMEM((verts, slots, width, edge), jnp.bfloat16),

time: 27.8 us -> 26.9 us (0.968)
  Pallas kernels: 25.4 us -> 24.5 us
    pallas_call x1, Pallas kernels: 25.4 us -> 24.5 us  [per_device(): pl.pallas_call(functools.partial(exchange_kernel, dims), out_shape=jax.Sh...]
where the time goes in v3:
time: 26.9 us; the launch traced here: 26.7 us
  Pallas kernels  24.5 us (91%)
  matrix products  2.19 us (8%)
    pallas_call x1, Pallas kernels, per_device(): pl.pallas_call(functools.partial(exchange_kernel, dims), out_shape=jax.Sh...  24.5 us
    dot_general x1, matrix products, per_device(): lax.dot_general(gathered, weight, (((0,), (0,)), ((), ())), preferred_ele...  2.19 us

profile of v3, /device:TPU:0, one launch (start us, length us, event | category | flops | bytes accessed | tf_op | source)
XLA Modules:
  0.0 26.7 jit_solution(3425112026443075101)
XLA Ops:
  0.0 0.0 copy-start
  0.0 0.0 copy-start.1
  0.0 24.5 %shard_map.73 = bf16[256,1024]{1,0:T(8,128)(2,1)} custom-call(s32[16,64]{1,0:T(8,128)} %bitcast.5, s32[64]{0:T(128)} %count_in.1, s32[1,4,4]{2,1,0:T(4,128)} %send_in.1, bf16[32,8192]{1,0:T(8,128)(2,1)} %bitcast.4, bf16[64,16,128,128]{3,2,1,0:T(8,128)(2,1)} %tiles.1), custom_call_target="tpu_custom_call" | custom-call | tf_op jit(solution)/shard_map/pallas_call | solution.py:166
  24.5 0.0 copy-done
  24.5 0.0 copy-done.1
  24.5 2.2 %fusion.1 = bf16[1024,256]{1,0:T(8,128)(2,1)} fusion(bf16[256,1024]{1,0:T(8,128)(2,1)} %shard_map.73, bf16[256,256]{1,0:T(8,128)(2,1)S(1)} %copy-done, f32[256]{0:T(256)S(1)} %copy-done.1), kind=kOutput, calls=%fused_computation.2 | convolution fusion | flops 135004160 | bytes 1180672 | tf_op jit(solution)/shard_map/dot_general | solution.py:199
Async XLA Ops:
  0.0 24.5 %copy-start = (bf16[256,256]{1,0:T(8,128)(2,1)S(1)}, bf16[256,256]{1,0:T(8,128)(2,1)}, u32[]{:S(2)}) copy-start(bf16[256,256]{1,0:T(8,128)(2,1)} %param.12) | copy-start | bytes 393220
  0.0 24.5 %copy-start.1 = (f32[256]{0:T(256)S(1)}, f32[256]{0:T(256)}, u32[]{:S(2)}) copy-start(f32[256]{0:T(256)} %param.13) | copy-start | bytes 3076
